TPU v7x, 32 devices: a whole 2x2x4 slice. The times are simulated.
32 devices in a mesh: dp: 8 (over z, y), tensor: 4 (over x, core).
Axes of the slice: x: 2, y: 2, z: 4, core: 2. Of those that a mesh axis runs over, the one named last changes fastest.
Arguments:
- hidden: bfloat16 [4096, 5120], P('dp'), may hold values from -48 to 48
- head_weight: bfloat16 [5120, 4096], P(None, 'tensor'), may hold values from -0.069877124 to 0.069877124
- token_ids: int32 [4096], P('dp'), may hold values from 0 to 4095
- old_logprob: float32 [4096], P('dp'), may hold values from -12.5 to 0.3
- rewards: int32 [64], P('dp'), may hold values from 0 to 1, as said below
- lengths: int32 [64], P('dp'), may hold values from 1 to 64, as said below
- group_ids: int32 [64], P('dp'), may hold values from 0 to 3, as said below
- loss_scale: float32 [], replicated, may hold values from 4096 to 16384
Outputs:
- loss: float32 [], replicated
- grad_hidden: float32 [4096, 5120], P('dp', 'tensor')
- grad_weight: float32 [5120, 4096], P('dp', 'tensor')
Inputs may be any that keep to these rules, and one draw needn't show every extreme that they name: `group_ids`: each group number names exactly 16 rollouts. `rewards`: some group holds both a 0 and a 1. `lengths`: some index of dp holds only rollouts of length 64 whose prompts hold both a 0 and a 1.
All inputs are finite; a program needn't handle non-finite values.
Results may differ from a plain program's by a relative error of at most 0.003.
Values may be sent and summed in bfloat16 or wider, within the bound.
A program may use at most 192 MiB of HBM per device.

v0:
```python
import jax
import jax.numpy as jnp
from jax import lax
from jax.sharding import PartitionSpec as P

GROUP = 16
clip_low = 0.2
clip_high = 0.28


def contract_rows(first_operand, second_operand):
    return lax.dot_general(
        first_operand, second_operand, (((0,), (0,)), ((), ())), preferred_element_type=jnp.float32
    )


def contract_cols(first_operand, second_operand):
    return lax.dot_general(
        first_operand, second_operand, (((1,), (1,)), ((), ())), preferred_element_type=jnp.float32
    )


def run_blocks(block_fn, initial):
    return block_fn(0, initial)


def group_terms(member, group_wins, reward_float):
    group_alive = jnp.logical_and(group_wins > 0.5, group_wins < GROUP - 0.5).astype(jnp.float32)
    center = group_wins / GROUP
    spread = jnp.where(group_alive > 0.5, jnp.sqrt(group_wins * (GROUP - group_wins)) / GROUP, 1.0)
    roll_alive = jnp.sum(member * group_alive[None, :], axis=1)
    roll_center = jnp.sum(member * center[None, :], axis=1)
    roll_spread = jnp.sum(member * spread[None, :], axis=1)
    advantage = roll_alive * (reward_float - roll_center) / roll_spread
    return (group_alive, roll_alive, advantage)


def policy_terms(log_prob, old_rows, adv_rows, weight_rows, factor):
    prob_ratio = jnp.exp(log_prob - old_rows)
    clipped = jnp.clip(prob_ratio, 1.0 - clip_low, 1.0 + clip_high)
    token_loss = -jnp.minimum(prob_ratio * adv_rows, clipped * adv_rows)
    active = prob_ratio * adv_rows <= clipped * adv_rows
    coefficient = jnp.where(active, -adv_rows * prob_ratio, 0.0) * weight_rows * factor
    return (token_loss, coefficient)


def shards(hidden, head_weight, token_ids, old_logprob, rewards, lengths, group_ids, loss_scale):
    row_count, model_width = hidden.shape
    roll_count = rewards.shape[0]
    response = row_count // roll_count
    vocab_part = head_weight.shape[1]
    data_size = lax.axis_size("dp")
    group_count = roll_count * data_size // GROUP
    member = (group_ids[:, None] == jnp.arange(group_count, dtype=jnp.int32)[None, :]).astype(
        jnp.float32
    )
    reward_float = rewards.astype(jnp.float32)
    length_float = lengths.astype(jnp.float32)
    local_wins = jnp.sum(member * reward_float[:, None], axis=0)
    group_wins = lax.psum(local_wins, "dp")
    group_alive, roll_alive, advantage = group_terms(member, group_wins, reward_float)
    token_count = lax.psum(jnp.sum(roll_alive * length_float), "dp")
    divisor = jnp.maximum(token_count, 1.0)
    factor = loss_scale / divisor
    position = jnp.arange(response, dtype=jnp.int32)
    inside = (position[None, :] < lengths[:, None]).astype(jnp.float32)
    token_weight = (roll_alive[:, None] * inside).reshape(row_count)
    token_adv = jnp.broadcast_to(advantage[:, None], (roll_count, response)).reshape(row_count)

    def logit_block(block_index, current):
        block_logits = jnp.dot(hidden, head_weight, preferred_element_type=jnp.float32)
        return block_logits

    logits = run_blocks(logit_block, jnp.zeros((row_count, vocab_part), jnp.float32))
    row_top = lax.pmax(jnp.max(logits, axis=1), "tensor")
    shifted = jnp.exp(logits - row_top[:, None])
    column = (
        jnp.arange(vocab_part, dtype=jnp.int32)[None, :] + lax.axis_index("tensor") * vocab_part
    )
    is_target = column == token_ids[:, None]
    row_total, target = lax.psum(
        (jnp.sum(shifted, axis=1), jnp.sum(jnp.where(is_target, logits, 0.0), axis=1)), "tensor"
    )
    softmax_rows = shifted / row_total[:, None]
    log_prob = target - row_top - jnp.log(row_total)
    token_loss, coefficient = policy_terms(log_prob, old_logprob, token_adv, token_weight, factor)
    logit_grad = (coefficient[:, None] * (is_target.astype(jnp.float32) - softmax_rows)).astype(
        jnp.bfloat16
    )

    def grad_block(block_index, current):
        return contract_cols(logit_grad, head_weight)

    grad_part = run_blocks(grad_block, jnp.zeros((row_count, model_width), jnp.float32))
    columns = lax.all_to_all(hidden, "dp", split_axis=1, concat_axis=0, tiled=True)
    grad_weight = contract_rows(columns, lax.all_gather(logit_grad, "dp", axis=0, tiled=True))
    grad_cols = lax.psum_scatter(grad_part, "tensor", scatter_dimension=1, tiled=True)
    loss_total = lax.psum(jnp.sum(token_weight * token_loss), "dp")
    return (loss_total / divisor, grad_cols, grad_weight)


def solution(mesh):
    return jax.shard_map(
        shards,
        mesh=mesh,
        in_specs=(
            P("dp", None),
            P(None, "tensor"),
            P("dp"),
            P("dp"),
            P("dp"),
            P("dp"),
            P("dp"),
            P(),
        ),
        out_specs=(P(), P("dp", "tensor"), P("dp", "tensor")),
        check_vma=False,
    )
```

profile of v0, /device:TPU:4, one launch (start us, length us, event | category | flops | bytes accessed | tf_op | source)
XLA Modules:
  0.0 332.5 jit_solution(15351003358301694592)
XLA Ops:
  8.0 0.0 all-gather.2.cloned.1.call-start
  8.0 0.7 convert_element_type.17
  8.7 0.8 select_reduce_fusion.3
  9.5 18.0 %psum.35 = f32[4]{0:T(128)S(1)} all-reduce(f32[4]{0:T(128)S(1)} %select_reduce_fusion.3), channel_id=1, replica_groups=mesh['dp'=8,'tensor'=4] {'dp'}, use_global_device_ids=true, to_apply=%region_1.0 | all-reduce | flops 4 | bytes 32 | tf_op jit(solution)/shard_map/psum | solution.py:60
  28.1 0.7 select_reduce_fusion.1
  28.9 0.7 fusion.5
  29.6 1.3 multiply_reduce_fusion.1
  30.9 0.1 broadcast_in_dim.12
  30.9 0.1 reshape.36
  31.0 0.1 mul.91
  31.1 0.0 copy-start
  31.1 0.0 copy-start.1
  31.1 10.0 %fusion.8 = (f32[512]{0:T(512)S(1)}, f32[512,1024]{1,0:T(8,128)S(1)}) fusion(bf16[512,5120]{1,0:T(8,128)(2,1)} %param.8, bf16[5120,1024]{1,0:T(8,128)(2,1)} %param.9), kind=kOutput, calls=%fused_computation.29 | convolution fusion | flops 5369232896 | bytes 17827840 | tf_op jit(solution)/shard_map/dot_general | solution.py:71
  41.1 5.7 %pmax.7 = f32[512]{0:T(512)S(1)} all-reduce(f32[512]{0:T(512)S(1)} %get-tuple-element.30), channel_id=1, replica_groups=mesh['dp'=8,'tensor'=4] {'tensor'}, use_global_device_ids=true, to_apply=%region_6.7 | all-reduce | flops 512 | bytes 4096 | tf_op jit(solution)/shard_map/pmax | solution.py:75
  46.8 0.0 copy-done
  46.8 0.7 fusion
  47.5 6.6 %all-reduce.1 = (f32[512]{0:T(512)S(1)}, f32[512]{0:T(512)S(1)}) all-reduce(f32[512]{0:T(512)S(1)} %get-tuple-element.16, f32[512]{0:T(512)S(1)} %get-tuple-element.15), channel_id=1, replica_groups=mesh['dp'=8,'tensor'=4] {'tensor'}, use_global_device_ids=true, to_apply=%region_8.9 | all-reduce | flops 1024 | bytes 8192 | tf_op jit(solution)/shard_map/psum | solution.py:81
  54.1 0.0 copy-done.1
  54.1 0.6 multiply_reduce_fusion
  54.7 22.0 %all-reduce = (f32[]{:T(128)}, f32[]{:T(128)}) all-reduce(f32[]{:T(128)} %get-tuple-element.24, f32[]{:T(128)} %get-tuple-element.26), channel_id=1, replica_groups=mesh['dp'=8,'tensor'=4] {'dp'}, use_global_device_ids=true, to_apply=%region_12.13 | all-reduce | flops 2 | bytes 16 | tf_op jit(solution)/shard_map/psum | solution.py:98
  77.4 1.6 fusion.3
  79.1 0.0 all-gather.2.cloned.1.call-update
  79.1 0.0 reduce-scatter.2.cloned.1.call-start
  79.2 10.9 %fusion.9 = f32[512,5120]{1,0:T(8,128)} fusion(bf16[512,1024]{1,0:T(8,128)(2,1)} %fusion.3, bf16[5120,1024]{1,0:T(8,128)(2,1)} %param.9), kind=kOutput, calls=%fused_computation.30 | convolution fusion | flops 5368709120 | bytes 22020096 | tf_op jit(solution)/shard_map/dot_general | solution.py:18
  90.1 0.0 reduce-scatter.2.cloned.1.call-update
  90.1 8.2 %copy.16 = bf16[512,5120]{0,1:T(8,128)(2,1)} copy(bf16[512,5120]{1,0:T(8,128)(2,1)} %param.8) | data formatting | bytes 10485760 | tf_op args[0]
  98.3 4.8 %all-to-all-start = ((bf16[512,8,640]{0,2,1:T(8,128)(2,1)}), bf16[512,8,640]{0,2,1:T(8,128)(2,1)}, u32[]{:S(2)}, u32[]{:S(2)}) async-start(bf16[512,8,640]{0,2,1:T(8,128)(2,1)} %bitcast.11), calls=%async_computation.1 | async-start | bytes 10485760 | tf_op jit(solution)/shard_map/all_to_all | solution.py:95
  103.8 199.4 %all-to-all-done = bf16[512,8,640]{0,2,1:T(8,128)(2,1)} async-done(((bf16[512,8,640]{0,2,1:T(8,128)(2,1)}), bf16[512,8,640]{0,2,1:T(8,128)(2,1)}, u32[]{:S(2)}, u32[]{:S(2)}) %all-to-all-start) | async-done | bytes 5242912 | tf_op jit(solution)/shard_map/all_to_all | solution.py:95
  303.2 7.9 %copy.17 = bf16[8,512,640]{2,1,0:T(8,128)(2,1)} copy(bf16[8,512,640]{1,2,0:T(8,128)(2,1)} %bitcast.1) | data formatting | bytes 10485760 | tf_op jit(solution)/shard_map/all_to_all | solution.py:95
  311.1 0.0 all-gather.2.cloned.1.call-done
  311.1 10.7 %convolution_bitcast_fusion = f32[640,1024]{0,1:T(8,128)S(1)} fusion(bf16[4096,1024]{1,0:T(8,128)(2,1)} %all-gather.2.cloned.1.call-done, bf16[4096,640]{1,0:T(8,128)(2,1)} %bitcast.12), kind=kOutput, calls=%fused_computation.8 | convolution fusion | flops 5368709120 | bytes 16252928 | tf_op jit(solution)/shard_map/dot_general | solution.py:12
  321.8 2.1 copy.18
  323.9 0.0 reduce-scatter.2.cloned.1.call-done
  (4 shorter events, 0.0 us)
Async XLA Ops:
  8.0 303.1 %all-gather.2.cloned.1.call-start = ((), (), s32[]{:S(2)}) async-start(), calls=%async_computation.3 | async-start | bytes 9437184 | tf_op jit(solution)/shard_map/all_gather | solution.py:96
  31.1 15.7 %copy-start = (s32[512]{0:T(512)S(1)}, s32[512]{0:T(512)}, u32[]{:S(2)}) copy-start(s32[512]{0:T(512)} %param.10) | copy-start | bytes 6148
  31.1 23.0 %copy-start.1 = (f32[512]{0:T(512)S(1)}, f32[512]{0:T(512)}, u32[]{:S(2)}) copy-start(f32[512]{0:T(512)} %param.11) | copy-start | bytes 6148
  79.1 244.8 %reduce-scatter.2.cloned.1.call-start = ((), (), s32[]{:S(2)}) async-start(), calls=%async_computation.2 | async-start | bytes 13107200 | tf_op jit(solution)/shard_map/reduce_scatter | solution.py:97
  98.3 204.9 %all-to-all-start = ((bf16[512,8,640]{0,2,1:T(8,128)(2,1)}), bf16[512,8,640]{0,2,1:T(8,128)(2,1)}, u32[]{:S(2)}, u32[]{:S(2)}) async-start(bf16[512,8,640]{0,2,1:T(8,128)(2,1)} %bitcast.11), calls=%async_computation.1 | async-start | bytes 10485760 | tf_op jit(solution)/shard_map/all_to_all | solution.py:95
Sparse Core Ops, SparseCore 0:
  79.2 219.8 all-gather.1
Sparse Core Ops, SparseCore 1:
  90.2 81.7 reduce-scatter.1
where the time goes:
time: 333 us; the launch traced here: 332 us
  waiting for transfers between devices  199 us (60%)
  blocking collectives  52.3 us (16%)
  matrix products  31.7 us (10%)
  between operations  18.7 us (6%)
  local copies, waits for them, and re-layouts  18.4 us (6%)
  other arithmetic  7.13 us (2%)
  starting transfers between devices  4.89 us (1%)
    all_to_all x1, waiting for transfers between devices, shards(): lax.all_to_all(hidden, 'dp', split_axis=1, concat_axis=0, tiled=True)  199 us
    psum x1, blocking collectives, shards(): loss_total = lax.psum(jnp.sum(token_weight * token_loss), 'dp')  22 us
    psum x1, blocking collectives, shards(): group_wins = lax.psum(local_wins, 'dp')  18 us
    dot_general x1, matrix products, contract_cols(): lax.dot_general(first_operand, second_operand, (((1,), (1,)), ((), ())),...  10.9 us
    dot_general x1, matrix products, contract_rows(): lax.dot_general(first_operand, second_operand, (((0,), (0,)), ((), ())),...  10.7 us
    unnamed x6, local copies, waits for them, and re-layouts  10.3 us
    dot_general x1, matrix products, logit_block(): jnp.dot(hidden, head_weight, preferred_element_type=jnp.float32)  10 us
    all_to_all x1, local copies, waits for them, and re-layouts, shards(): lax.all_to_all(hidden, 'dp', split_axis=1, concat_axis=0, tiled=True)  7.87 us
  transfers between devices with their start and end apart: 3, of which 1 were waited for; matrix products, arithmetic and copies ran while one was open for 12% of the time, Pallas kernels for 0%

commit v1 on v0

--- a/solution.py
+++ b/solution.py
@@ -92,7 +92,9 @@
         return contract_cols(logit_grad, head_weight)
 
     grad_part = run_blocks(grad_block, jnp.zeros((row_count, model_width), jnp.float32))
-    columns = lax.all_to_all(hidden, "dp", split_axis=1, concat_axis=0, tiled=True)
+    parts = jnp.split(hidden, lax.axis_size("dp"), axis=1)
+    got = lax.all_to_all(jnp.stack(parts), "dp", 0, 0)
+    columns = jnp.concatenate(got, axis=0)
     grad_weight = contract_rows(columns, lax.all_gather(logit_grad, "dp", axis=0, tiled=True))
     grad_cols = lax.psum_scatter(grad_part, "tensor", scatter_dimension=1, tiled=True)
     loss_total = lax.psum(jnp.sum(token_weight * token_loss), "dp")

time: 333 us -> 325 us (0.976)
  waiting for transfers between devices: 199 us -> 191 us
    all_to_all x1, waiting for transfers between devices: 199 us -> 191 us  [shards(): got = lax.all_to_all(jnp.stack(parts), 'dp', 0, 0)]
    all_to_all x1 -> x0, local copies, waits for them, and re-layouts: 7.87 us -> none  [shards(): lax.all_to_all(hidden, 'dp', split_axis=1, concat_axis=0, tiled=True)]
    unnamed x6 -> x11, local copies, waits for them, and re-layouts: 10.3 us -> 14.7 us
where the time goes in v1:
time: 325 us; the launch traced here: 322 us
  waiting for transfers between devices  191 us (59%)
  blocking collectives  52.3 us (16%)
  matrix products  31.6 us (10%)
  between operations  18.7 us (6%)
  local copies, waits for them, and re-layouts  17 us (5%)
  other arithmetic  7.14 us (2%)
  starting transfers between devices  4.69 us (1%)
    all_to_all x1, waiting for transfers between devices, shards(): got = lax.all_to_all(jnp.stack(parts), 'dp', 0, 0)  191 us
    psum x1, blocking collectives, shards(): loss_total = lax.psum(jnp.sum(token_weight * token_loss), 'dp')  22 us
    psum x1, blocking collectives, shards(): group_wins = lax.psum(local_wins, 'dp')  18 us
    unnamed x11, local copies, waits for them, and re-layouts  14.7 us
    dot_general x1, matrix products, contract_cols(): lax.dot_general(first_operand, second_operand, (((1,), (1,)), ((), ())),...  10.9 us
    dot_general x1, matrix products, contract_rows(): lax.dot_general(first_operand, second_operand, (((0,), (0,)), ((), ())),...  10.6 us
    dot_general x1, matrix products, logit_block(): jnp.dot(hidden, head_weight, preferred_element_type=jnp.float32)  10 us
    psum x1, blocking collectives, shards(): lax.psum((jnp.sum(shifted, axis=1), jnp.sum(jnp.where(is_target, logits,...  6.62 us
  transfers between devices with their start and end apart: 3, of which 1 were waited for; matrix products, arithmetic and copies ran while one was open for 12% of the time, Pallas kernels for 0%

profile of v1, /device:TPU:4, one launch (start us, length us, event | category | flops | bytes accessed | tf_op | source)
XLA Modules:
  0.0 322.5 jit_solution(18044664308599387839)
XLA Ops:
  8.0 0.0 all-gather.2.cloned.1.call-start
  8.0 0.7 convert_element_type.17
  8.7 0.8 select_reduce_fusion.3
  9.5 18.0 %psum.35 = f32[4]{0:T(128)S(1)} all-reduce(f32[4]{0:T(128)S(1)} %select_reduce_fusion.3), channel_id=1, replica_groups=mesh['dp'=8,'tensor'=4] {'dp'}, use_global_device_ids=true, to_apply=%region_1.0 | all-reduce | flops 4 | bytes 32 | tf_op jit(solution)/shard_map/psum | solution.py:60
  27.5 0.7 select_reduce_fusion.1
  28.2 0.7 fusion.5
  28.9 0.1 mul.91
  29.0 1.3 multiply_reduce_fusion.1
  30.3 0.1 broadcast_in_dim.12
  30.4 0.1 reshape.36
  30.4 0.0 copy-start
  30.4 0.0 copy-start.1
  30.4 10.0 %fusion.8 = (f32[512]{0:T(512)S(1)}, f32[512,1024]{1,0:T(8,128)S(1)}) fusion(bf16[512,5120]{1,0:T(8,128)(2,1)} %param.8, bf16[5120,1024]{1,0:T(8,128)(2,1)} %param.9), kind=kOutput, calls=%fused_computation.36 | convolution fusion | flops 5369232896 | bytes 17827840 | tf_op jit(solution)/shard_map/dot_general | solution.py:71
  40.5 5.7 %pmax.7 = f32[512]{0:T(512)S(1)} all-reduce(f32[512]{0:T(512)S(1)} %get-tuple-element.18), channel_id=1, replica_groups=mesh['dp'=8,'tensor'=4] {'tensor'}, use_global_device_ids=true, to_apply=%region_6.7 | all-reduce | flops 512 | bytes 4096 | tf_op jit(solution)/shard_map/pmax | solution.py:75
  46.8 0.0 copy-done
  46.8 0.7 fusion
  47.5 6.6 %all-reduce.1 = (f32[512]{0:T(512)S(1)}, f32[512]{0:T(512)S(1)}) all-reduce(f32[512]{0:T(512)S(1)} %get-tuple-element.4, f32[512]{0:T(512)S(1)} %get-tuple-element.3), channel_id=1, replica_groups=mesh['dp'=8,'tensor'=4] {'tensor'}, use_global_device_ids=true, to_apply=%region_8.9 | all-reduce | flops 1024 | bytes 8192 | tf_op jit(solution)/shard_map/psum | solution.py:81
  54.1 0.0 copy-done.1
  54.1 0.6 multiply_reduce_fusion
  54.7 22.0 %all-reduce = (f32[]{:T(128)}, f32[]{:T(128)}) all-reduce(f32[]{:T(128)} %get-tuple-element.12, f32[]{:T(128)} %get-tuple-element.14), channel_id=1, replica_groups=mesh['dp'=8,'tensor'=4] {'dp'}, use_global_device_ids=true, to_apply=%region_12.13 | all-reduce | flops 2 | bytes 16 | tf_op jit(solution)/shard_map/psum | solution.py:100
  77.5 1.6 fusion.3
  79.1 0.0 all-gather.2.cloned.1.call-update
  79.1 0.0 reduce-scatter.2.cloned.1.call-start
  79.2 10.9 %fusion.9 = f32[512,5120]{1,0:T(8,128)} fusion(bf16[512,1024]{1,0:T(8,128)(2,1)} %fusion.3, bf16[5120,1024]{1,0:T(8,128)(2,1)} %param.9), kind=kOutput, calls=%fused_computation.37 | convolution fusion | flops 5368709120 | bytes 22020096 | tf_op jit(solution)/shard_map/dot_general | solution.py:18
  90.1 0.0 reduce-scatter.2.cloned.1.call-update
  90.1 2.0 bitcast_dynamic-update-slice_fusion.7
  92.1 2.0 bitcast_dynamic-update-slice_fusion.6
  94.1 2.1 bitcast_dynamic-update-slice_fusion.5
  96.2 2.2 bitcast_dynamic-update-slice_fusion.4
  98.4 2.2 bitcast_dynamic-update-slice_fusion.3
  100.6 2.2 bitcast_dynamic-update-slice_fusion.2
  102.8 2.1 bitcast_dynamic-update-slice_fusion.1
  104.8 2.0 bitcast_dynamic-update-slice_fusion
  106.9 4.6 %all-to-all-start = ((bf16[8,512,640]{2,1,0:T(8,128)(2,1)}), bf16[8,512,640]{2,1,0:T(8,128)(2,1)}, u32[]{:S(2)}, u32[]{:S(2)}) async-start(bf16[8,512,640]{2,1,0:T(8,128)(2,1)} %bitcast_dynamic-update-slice_fusion), calls=%async_computation.1 | async-start | bytes 10485760 | tf_op jit(solution)/shard_map/all_to_all | solution.py:96
  112.2 191.1 %all-to-all-done = bf16[8,512,640]{2,1,0:T(8,128)(2,1)} async-done(((bf16[8,512,640]{2,1,0:T(8,128)(2,1)}), bf16[8,512,640]{2,1,0:T(8,128)(2,1)}, u32[]{:S(2)}, u32[]{:S(2)}) %all-to-all-start) | async-done | bytes 5242912 | tf_op jit(solution)/shard_map/all_to_all | solution.py:96
  303.3 0.0 all-gather.2.cloned.1.call-done
  303.3 10.6 %fusion.10 = f32[640,1024]{1,0:T(8,128)} fusion(bf16[4096,640]{1,0:T(8,128)(2,1)} %bitcast.8, bf16[4096,1024]{1,0:T(8,128)(2,1)} %all-gather.2.cloned.1.call-done), kind=kOutput, calls=%fused_computation.38 | convolution fusion | flops 5368709120 | bytes 16252928 | tf_op jit(solution)/shard_map/dot_general | solution.py:12
  313.9 0.0 reduce-scatter.2.cloned.1.call-done
  (4 shorter events, 0.0 us)
Async XLA Ops:
  8.0 295.3 %all-gather.2.cloned.1.call-start = ((), (), s32[]{:S(2)}) async-start(), calls=%async_computation.3 | async-start | bytes 9437184 | tf_op jit(solution)/shard_map/all_gather | solution.py:98
  30.4 16.4 %copy-start = (s32[512]{0:T(512)S(1)}, s32[512]{0:T(512)}, u32[]{:S(2)}) copy-start(s32[512]{0:T(512)} %param.10) | copy-start | bytes 6148
  30.4 23.7 %copy-start.1 = (f32[512]{0:T(512)S(1)}, f32[512]{0:T(512)}, u32[]{:S(2)}) copy-start(f32[512]{0:T(512)} %param.11) | copy-start | bytes 6148
  79.1 234.8 %reduce-scatter.2.cloned.1.call-start = ((), (), s32[]{:S(2)}) async-start(), calls=%async_computation.2 | async-start | bytes 13107200 | tf_op jit(solution)/shard_map/reduce_scatter | solution.py:99
  106.9 196.4 %all-to-all-start = ((bf16[8,512,640]{2,1,0:T(8,128)(2,1)}), bf16[8,512,640]{2,1,0:T(8,128)(2,1)}, u32[]{:S(2)}, u32[]{:S(2)}) async-start(bf16[8,512,640]{2,1,0:T(8,128)(2,1)} %bitcast_dynamic-update-slice_fusion), calls=%async_computation.1 | async-start | bytes 10485760 | tf_op jit(solution)/shard_map/all_to_all | solution.py:96
Sparse Core Ops, SparseCore 0:
  79.2 216.8 all-gather.1
Sparse Core Ops, SparseCore 1:
  90.2 81.7 reduce-scatter.1
